TPU v7x, 32 devices: a whole 2x2x4 slice. The times are simulated.
32 devices in a mesh: ep: 4 (over y, x), fsdp: 8 (over z, core).
Axes of the slice: x: 2, y: 2, z: 4, core: 2. Of those that a mesh axis runs over, the one named last changes fastest.
Arguments:
- train_gate: float32 [64, 2048, 1408], P('ep', 'fsdp'), may hold values from -0.1875 to 0.1875
- train_up: float32 [64, 2048, 1408], P('ep', 'fsdp'), may hold values from -0.1875 to 0.1875
- train_down: float32 [64, 1408, 2048], P('ep', None, 'fsdp'), may hold values from -0.21875 to 0.21875
- router_weight: float32 [2048, 64], P('fsdp', 'ep'), may hold values from -0.125 to 0.125
- router_gain: float32 [2048], P('fsdp'), may hold values from 0.25 to 1.75
Outputs:
- ready_gate: bfloat16 [64, 2048, 1408], P('ep', None, 'fsdp')
- ready_up: bfloat16 [64, 2048, 1408], P('ep', None, 'fsdp')
- ready_down: bfloat16 [64, 1408, 2048], P('ep', 'fsdp')
- scale_gate: float32 [64, 1408], P('ep', 'fsdp')
- scale_up: float32 [64, 1408], P('ep', 'fsdp')
- scale_down: float32 [64, 1408], P('ep', 'fsdp')
- serve_router: bfloat16 [2048, 64], replicated
All inputs are finite; a program needn't handle non-finite values. Where the computation divides by a largest or mean magnitude, that divisor is 1e-20 or more.
Results may differ from a plain program's by a relative error of at most 0.001.
Values may be sent and summed in bfloat16 or wider, within the bound.
A program may use at most 256 MiB of HBM per device.

v0:
```python
import jax
import jax.numpy as jnp
from jax import lax
from jax.sharding import PartitionSpec as P


def per_device(train_gate, train_up, train_down, router_weight, router_gain):
    scale_gate, scale_up, scale_down = lax.pmax(
        (
            jnp.max(jnp.abs(train_gate), axis=1),
            jnp.max(jnp.abs(train_up), axis=1),
            jnp.max(jnp.abs(train_down), axis=2),
        ),
        "fsdp",
    )
    narrow_gate, narrow_up, narrow_down = (
        (train_gate / jnp.expand_dims(scale_gate, 1)).astype(jnp.bfloat16),
        (train_up / jnp.expand_dims(scale_up, 1)).astype(jnp.bfloat16),
        (train_down / jnp.expand_dims(scale_down, 2)).astype(jnp.bfloat16),
    )
    ready_gate, ready_up = (
        lax.all_to_all(narrow_gate, "fsdp", split_axis=2, concat_axis=1, tiled=True),
        lax.all_to_all(narrow_up, "fsdp", split_axis=2, concat_axis=1, tiled=True),
    )
    ready_down = lax.all_to_all(narrow_down, "fsdp", split_axis=1, concat_axis=2, tiled=True)
    scale_gate = lax.dynamic_slice_in_dim(
        scale_gate, lax.axis_index("fsdp") * ready_gate.shape[2], ready_gate.shape[2], axis=1
    )
    scale_up = lax.dynamic_slice_in_dim(
        scale_up, lax.axis_index("fsdp") * ready_up.shape[2], ready_up.shape[2], axis=1
    )
    scale_down = lax.dynamic_slice_in_dim(
        scale_down, lax.axis_index("fsdp") * ready_down.shape[1], ready_down.shape[1], axis=1
    )
    part_router = (router_weight * router_gain[:, None]).astype(jnp.bfloat16)
    row_router = lax.all_gather(part_router, "fsdp", axis=0, tiled=True)
    serve_router = lax.all_gather(row_router, "ep", axis=1, tiled=True)
    return (ready_gate, ready_up, ready_down, scale_gate, scale_up, scale_down, serve_router)


def solution(mesh):
    placed = (
        P("ep", "fsdp", None),
        P("ep", "fsdp", None),
        P("ep", None, "fsdp"),
        P("fsdp", "ep"),
        P("fsdp"),
    )
    return jax.shard_map(
        per_device,
        mesh=mesh,
        in_specs=placed,
        out_specs=(
            P("ep", None, "fsdp"),
            P("ep", None, "fsdp"),
            P("ep", "fsdp", None),
            P("ep", "fsdp"),
            P("ep", "fsdp"),
            P("ep", "fsdp"),
            P(),
        ),
        check_vma=False,
    )
```

profile of v0, /device:TPU:0, one launch (start us, length us, event | category | flops | bytes accessed | tf_op | source)
XLA Modules:
  0.0 985.2 jit_solution(7565016768209817902)
XLA Ops:
  7.2 0.0 all-reduce.3.cloned.1.call-start
  7.2 0.0 slice-start
  7.2 0.0 slice-start.1
  7.2 0.0 slice-start.2
  7.2 10.5 %abs_reduce_fusion = f32[16,1408]{1,0:T(8,128)} fusion(f32[16,1408,256]{2,1,0:T(8,128)} %param.7), kind=kLoop, calls=%fused_computation.2 | loop fusion | flops 11511808 | bytes 23158784 | tf_op jit(solution)/shard_map/reduce_max | solution.py:12
  17.7 0.0 slice-start.3
  17.7 0.0 slice-start.4
  17.7 0.0 slice-start.5
  17.7 10.8 %abs_reduce_fusion.1 = f32[16,1408]{1,0:T(8,128)} fusion(f32[16,256,1408]{2,1,0:T(8,128)} %param.6), kind=kLoop, calls=%fused_computation.4 | loop fusion | flops 11511808 | bytes 23158784 | tf_op jit(solution)/shard_map/reduce_max | solution.py:11
  28.5 0.0 slice-done
  28.5 0.0 slice-done.1
  28.6 0.0 slice-done.2
  28.6 0.0 slice-done.3
  28.6 0.0 slice-done.4
  28.6 0.0 slice-done.5
  28.6 2.4 abs_reduce_fusion.2
  31.0 0.0 all-reduce.3.cloned.1.call-update
  31.0 23.7 %copy.24 = f32[16,256,1408]{1,0,2:T(8,128)} copy(f32[16,256,1408]{2,1,0:T(8,128)} %param.5) | data formatting | bytes 46137344 | tf_op args[0]
  54.7 32.5 %all-reduce.3.cloned.1.call-done = (f32[16,1408]{1,0:T(8,128)}, f32[16,1408]{1,0:T(8,128)}, f32[16,1408]{1,0:T(8,128)}) async-done(((f32[16,1408]{1,0:T(8,128)}, f32[16,1408]{1,0:T(8,128)}, f32[16,1408]{1,0:T(8,128)}), (f32[16,1408]{1,0:T(8,128)}, f32[16,1408]{1,0:T(8,128)}, f32[16,1408]{1,0:T(8,128)})) %all-reduce.3.cloned.1.call-update) | async-done | bytes 270352 | tf_op jit(solution)/shard_map/pmax | solution.py:8
  87.2 1.1 copy.23
  88.4 14.2 %divide_convert_fusion.1 = bf16[16,256,1408]{1,0,2:T(8,128)(2,1)} fusion(f32[16,256,1408]{1,0,2:T(8,128)} %copy.24, f32[16,1408]{0,1:T(8,128)S(1)} %copy.23), kind=kLoop, calls=%fused_computation.5 | loop fusion | flops 11534336 | bytes 34693120 | tf_op jit(solution)/shard_map/convert_element_type | solution.py:17
  102.6 5.4 all-to-all-start
  108.0 0.0 copy-start
  108.0 23.7 %copy.28 = f32[16,256,1408]{1,0,2:T(8,128)} copy(f32[16,256,1408]{2,1,0:T(8,128)} %param.6) | data formatting | bytes 46137344 | tf_op args[1]
  131.7 0.0 copy-done
  131.7 0.3 copy.27
  132.0 0.0 copy-start.1
  132.0 14.2 %divide_convert_fusion = bf16[16,256,1408]{1,0,2:T(8,128)(2,1)} fusion(f32[16,256,1408]{1,0,2:T(8,128)} %copy.28, f32[16,1408]{0,1:T(8,128)S(1)} %copy.27), kind=kLoop, calls=%fused_computation.3 | loop fusion | flops 11534336 | bytes 34693120 | tf_op jit(solution)/shard_map/convert_element_type | solution.py:18
  146.2 213.1 %all-to-all-done = bf16[16,256,1408]{1,0,2:T(8,128)(2,1)} async-done(((bf16[16,256,1408]{1,0,2:T(8,128)(2,1)}), bf16[16,256,1408]{1,0,2:T(8,128)(2,1)}, u32[]{:S(2)}, u32[]{:S(2)}) %all-to-all-start) | async-done | bytes 11534368 | tf_op jit(solution)/shard_map/all_to_all | solution.py:22
  359.4 5.2 all-to-all-start.1
  364.6 0.0 copy-done.1
  364.6 0.3 copy.31
  364.9 0.0 copy-start.2
  364.9 0.0 copy-start.3
  364.9 32.6 %fusion = bf16[16,1408,256]{2,0,1:T(8,128)(2,1)} fusion(f32[16,1408,256]{2,1,0:T(8,128)} %param.7, f32[16,1408]{0,1:T(8,128)S(1)} %copy.31), kind=kLoop, calls=%fused_computation.1 | loop fusion | flops 11534336 | bytes 34693120 | tf_op jit(solution)/shard_map/convert_element_type | solution.py:19
  397.5 218.4 %all-to-all-done.1 = bf16[16,256,1408]{1,0,2:T(8,128)(2,1)} async-done(((bf16[16,256,1408]{1,0,2:T(8,128)(2,1)}), bf16[16,256,1408]{1,0,2:T(8,128)(2,1)}, u32[]{:S(2)}, u32[]{:S(2)}) %all-to-all-start.1) | async-done | bytes 11534368 | tf_op jit(solution)/shard_map/all_to_all | solution.py:23
  615.9 5.3 all-to-all-start.2
  621.2 0.0 copy-done.2
  621.2 0.0 copy-done.3
  621.3 257.3 %all_gather.6 = bf16[2048,16]{0,1:T(8,128)(2,1)S(1)} all-gather(bf16[256,16]{0,1:T(8,128)(2,1)S(1)} %multiply_convert_fusion), channel_id=1, replica_groups=mesh['ep'=4,'fsdp'=8] {'fsdp'}, dimensions={0}, use_global_device_ids=true | all-gather | bytes 73728 | tf_op jit(solution)/shard_map/all_gather | solution.py:36
  878.5 9.1 all_gather.7
  887.7 1.4 constant_dynamic-slice_fusion.2
  889.1 0.7 constant_dynamic-slice_fusion
  889.8 11.3 %copy.26 = bf16[16,8,256,176]{2,1,3,0:T(8,128)(2,1)} copy(bf16[16,8,256,176]{2,0,3,1:T(8,128)(2,1)} %bitcast.2) | data formatting | bytes 23068672 | tf_op jit(solution)/shard_map/all_to_all | solution.py:22
  901.1 18.0 %all_to_all.42 = bf16[16,2048,176]{1,2,0:T(8,128)(2,1)} reshape(bf16[16,8,256,176]{2,1,3,0:T(8,128)(2,1)} %copy.26) | data formatting | bytes 23068672 | tf_op jit(solution)/shard_map/all_to_all | solution.py:22
  919.1 11.3 %copy.30 = bf16[16,8,256,176]{2,1,3,0:T(8,128)(2,1)} copy(bf16[16,8,256,176]{2,0,3,1:T(8,128)(2,1)} %bitcast.5) | data formatting | bytes 23068672 | tf_op jit(solution)/shard_map/all_to_all | solution.py:23
  930.4 18.0 %all_to_all.46 = bf16[16,2048,176]{1,2,0:T(8,128)(2,1)} reshape(bf16[16,8,256,176]{2,1,3,0:T(8,128)(2,1)} %copy.30) | data formatting | bytes 23068672 | tf_op jit(solution)/shard_map/all_to_all | solution.py:23
  948.4 0.0 all-to-all-done.2
  948.4 11.4 %copy.33 = bf16[16,176,8,256]{3,2,1,0:T(8,128)(2,1)} copy(bf16[16,176,8,256]{3,0,1,2:T(8,128)(2,1)} %bitcast.7) | data formatting | bytes 23068672 | tf_op jit(solution)/shard_map/all_to_all | solution.py:25
  959.7 18.0 %all_to_all.50 = bf16[16,176,2048]{2,1,0:T(8,128)(2,1)} reshape(bf16[16,176,8,256]{3,2,1,0:T(8,128)(2,1)} %copy.33) | data formatting | bytes 23068672 | tf_op jit(solution)/shard_map/all_to_all | solution.py:25
  977.7 0.7 copy.43
  (2 shorter events, 0.0 us)
Async XLA Ops:
  7.2 80.1 %all-reduce.3.cloned.1.call-start = ((), (), s32[]{:S(2)}) async-start(), calls=%async_computation.3 | async-start | bytes 540672 | tf_op jit(solution)/shard_map/pmax | solution.py:8
  7.2 21.3 %slice-start = ((s8[23068672]{0:T(1024)(128)(4,1)}), s8[4194304]{0:T(1024)(128)(4,1)S(1)}, s32[]{:S(2)}) async-start(s8[23068672]{0:T(1024)(128)(4,1)} %bitcast.19), calls=%async_computation.4 | async-start | bytes 8388608
  7.2 21.3 %slice-start.1 = ((s8[23068672]{0:T(1024)(128)(4,1)}), s8[4194304]{0:T(1024)(128)(4,1)S(1)}, s32[]{:S(2)}) async-start(s8[23068672]{0:T(1024)(128)(4,1)} %bitcast.19), calls=%async_computation.5 | async-start | bytes 8388608
  7.2 21.3 %slice-start.2 = ((s8[23068672]{0:T(1024)(128)(4,1)}), s8[4194304]{0:T(1024)(128)(4,1)S(1)}, s32[]{:S(2)}) async-start(s8[23068672]{0:T(1024)(128)(4,1)} %bitcast.19), calls=%async_computation.6 | async-start | bytes 8388608
  17.7 10.8 %slice-start.3 = ((s8[23068672]{0:T(1024)(128)(4,1)}), s8[4194304]{0:T(1024)(128)(4,1)S(1)}, s32[]{:S(2)}) async-start(s8[23068672]{0:T(1024)(128)(4,1)} %bitcast.19), calls=%async_computation.7 | async-start | bytes 8388608
  17.7 10.8 %slice-start.4 = ((s8[23068672]{0:T(1024)(128)(4,1)}), s8[4194304]{0:T(1024)(128)(4,1)S(1)}, s32[]{:S(2)}) async-start(s8[23068672]{0:T(1024)(128)(4,1)} %bitcast.19), calls=%async_computation.8 | async-start | bytes 8388608
  17.7 10.9 %slice-start.5 = ((s8[23068672]{0:T(1024)(128)(4,1)}), s8[2097152]{0:T(1024)(128)(4,1)S(1)}, s32[]{:S(2)}) async-start(s8[23068672]{0:T(1024)(128)(4,1)} %bitcast.19), calls=%async_computation.9 | async-start | bytes 4194304
  102.6 256.8 %all-to-all-start = ((bf16[16,256,1408]{1,0,2:T(8,128)(2,1)}), bf16[16,256,1408]{1,0,2:T(8,128)(2,1)}, u32[]{:S(2)}, u32[]{:S(2)}) async-start(bf16[16,256,1408]{1,0,2:T(8,128)(2,1)} %divide_convert_fusion.1), calls=%async_computation | async-start | bytes 23068672 | tf_op jit(solution)/shard_map/all_to_all | solution.py:22
  108.0 23.7 %copy-start = (f32[16,1408]{1,0:T(8,128)S(1)}, f32[16,1408]{1,0:T(8,128)}, u32[]{:S(2)}) copy-start(f32[16,1408]{1,0:T(8,128)} %get-tuple-element.8) | copy-start | bytes 270340
  132.0 232.6 %copy-start.1 = (f32[16,1408]{1,0:T(8,128)S(1)}, f32[16,1408]{1,0:T(8,128)}, u32[]{:S(2)}) copy-start(f32[16,1408]{1,0:T(8,128)} %get-tuple-element.9) | copy-start | bytes 270340
  359.4 256.5 %all-to-all-start.1 = ((bf16[16,256,1408]{1,0,2:T(8,128)(2,1)}), bf16[16,256,1408]{1,0,2:T(8,128)(2,1)}, u32[]{:S(2)}, u32[]{:S(2)}) async-start(bf16[16,256,1408]{1,0,2:T(8,128)(2,1)} %divide_convert_fusion), calls=%async_computation.1 | async-start | bytes 23068672 | tf_op jit(solution)/shard_map/all_to_all | solution.py:23
  364.9 256.3 %copy-start.2 = (f32[256,16]{0,1:T(8,128)S(1)}, f32[256,16]{0,1:T(8,128)}, u32[]{:S(2)}) copy-start(f32[256,16]{0,1:T(8,128)} %param.8) | copy-start | bytes 49156
  364.9 256.3 %copy-start.3 = (f32[256]{0:T(256)S(1)}, f32[256]{0:T(256)}, u32[]{:S(2)}) copy-start(f32[256]{0:T(256)} %param.9) | copy-start | bytes 3076
  615.9 332.5 %all-to-all-start.2 = ((bf16[16,1408,256]{2,0,1:T(8,128)(2,1)}), bf16[16,1408,256]{2,0,1:T(8,128)(2,1)}, u32[]{:S(2)}, u32[]{:S(2)}) async-start(bf16[16,1408,256]{2,0,1:T(8,128)(2,1)} %fusion), calls=%async_computation.2 | async-start | bytes 23068672 | tf_op jit(solution)/shard_map/all_to_all | solution.py:25
Sparse Core Ops, SparseCore 0:
  31.1 56.0 all-reduce.2
where the time goes:
time: 988 us; the launch traced here: 985 us
  waiting for transfers between devices  464 us (47%)
  blocking collectives  266 us (27%)
  local copies, waits for them, and re-layouts  140 us (14%)
  other arithmetic  84.8 us (9%)
  starting transfers between devices  16 us (2%)
  between operations  14.2 us (1%)
    all_gather x1, blocking collectives, per_device(): row_router = lax.all_gather(part_router, 'fsdp', axis=0, tiled=True)  257 us
    all_to_all x1, waiting for transfers between devices, per_device(): lax.all_to_all(narrow_up, 'fsdp', split_axis=2, concat_axis=1, tiled=True)  218 us
    all_to_all x1, waiting for transfers between devices, per_device(): lax.all_to_all(narrow_gate, 'fsdp', split_axis=2, concat_axis=1, tiled=True)  213 us
    unnamed x23, local copies, waits for them, and re-layouts  48.2 us
    convert_element_type x1, other arithmetic, per_device(): (train_down / jnp.expand_dims(scale_down, 2)).astype(jnp.bfloat16)  32.6 us
    pmax x1, waiting for transfers between devices, per_device(): lax.pmax((jnp.max(jnp.abs(train_gate), axis=1), jnp.max(jnp.abs(train_up)...  32.5 us
    all_to_all x2, local copies, waits for them, and re-layouts, per_device(): lax.all_to_all(narrow_down, 'fsdp', split_axis=1, concat_axis=2, tiled=True)  29.3 us
    all_to_all x2, local copies, waits for them, and re-layouts, per_device(): lax.all_to_all(narrow_gate, 'fsdp', split_axis=2, concat_axis=1, tiled=True)  29.3 us
  transfers between devices with their start and end apart: 4, of which 3 were waited for; matrix products, arithmetic and copies ran while one was open for 12% of the time, Pallas kernels for 0%

commit v1 on v0

--- a/solution.py
+++ b/solution.py
@@ -34,7 +34,8 @@
     )
     part_router = (router_weight * router_gain[:, None]).astype(jnp.bfloat16)
     row_router = lax.all_gather(part_router, "fsdp", axis=0, tiled=True)
-    serve_router = lax.all_gather(row_router, "ep", axis=1, tiled=True)
+    blocks = lax.all_gather(row_router, "ep")
+    serve_router = jnp.concatenate(blocks, axis=1)
     return (ready_gate, ready_up, ready_down, scale_gate, scale_up, scale_down, serve_router)
 
 

time: 988 us -> 988 us (level)
    unnamed x23 -> x22, local copies, waits for them, and re-layouts: 48.2 us -> 47.5 us
where the time goes in v1:
time: 988 us; the launch traced here: 985 us
  waiting for transfers between devices  464 us (47%)
  blocking collectives  266 us (27%)
  local copies, waits for them, and re-layouts  140 us (14%)
  other arithmetic  84.8 us (9%)
  starting transfers between devices  16 us (2%)
  between operations  14.2 us (1%)
    all_gather x1, blocking collectives, per_device(): row_router = lax.all_gather(part_router, 'fsdp', axis=0, tiled=True)  257 us
    all_to_all x1, waiting for transfers between devices, per_device(): lax.all_to_all(narrow_up, 'fsdp', split_axis=2, concat_axis=1, tiled=True)  218 us
    all_to_all x1, waiting for transfers between devices, per_device(): lax.all_to_all(narrow_gate, 'fsdp', split_axis=2, concat_axis=1, tiled=True)  213 us
    unnamed x22, local copies, waits for them, and re-layouts  47.5 us
    convert_element_type x1, other arithmetic, per_device(): (train_down / jnp.expand_dims(scale_down, 2)).astype(jnp.bfloat16)  32.6 us
    pmax x1, waiting for transfers between devices, per_device(): lax.pmax((jnp.max(jnp.abs(train_gate), axis=1), jnp.max(jnp.abs(train_up)...  32.5 us
    all_to_all x2, local copies, waits for them, and re-layouts, per_device(): lax.all_to_all(narrow_down, 'fsdp', split_axis=1, concat_axis=2, tiled=True)  29.3 us
    all_to_all x2, local copies, waits for them, and re-layouts, per_device(): lax.all_to_all(narrow_gate, 'fsdp', split_axis=2, concat_axis=1, tiled=True)  29.3 us
  transfers between devices with their start and end apart: 4, of which 3 were waited for; matrix products, arithmetic and copies ran while one was open for 12% of the time, Pallas kernels for 0%

profile of v1, /device:TPU:0, one launch (start us, length us, event | category | flops | bytes accessed | tf_op | source)
XLA Modules:
  0.0 985.3 jit_solution(11771086698281584803)
XLA Ops:
  7.2 0.0 all-reduce.3.cloned.1.call-start
  7.2 0.0 slice-start
  7.2 0.0 slice-start.1
  7.2 0.0 slice-start.2
  7.2 10.5 %abs_reduce_fusion = f32[16,1408]{1,0:T(8,128)} fusion(f32[16,1408,256]{2,1,0:T(8,128)} %param.7), kind=kLoop, calls=%fused_computation.2 | loop fusion | flops 11511808 | bytes 23158784 | tf_op jit(solution)/shard_map/reduce_max | solution.py:12
  17.7 0.0 slice-start.3
  17.7 0.0 slice-start.4
  17.7 0.0 slice-start.5
  17.7 10.8 %abs_reduce_fusion.1 = f32[16,1408]{1,0:T(8,128)} fusion(f32[16,256,1408]{2,1,0:T(8,128)} %param.6), kind=kLoop, calls=%fused_computation.4 | loop fusion | flops 11511808 | bytes 23158784 | tf_op jit(solution)/shard_map/reduce_max | solution.py:11
  28.5 0.0 slice-done
  28.5 0.0 slice-done.1
  28.6 0.0 slice-done.2
  28.6 0.0 slice-done.3
  28.6 0.0 slice-done.4
  28.6 0.0 slice-done.5
  28.6 2.4 abs_reduce_fusion.2
  31.0 0.0 all-reduce.3.cloned.1.call-update
  31.0 23.7 %copy.27 = f32[16,256,1408]{1,0,2:T(8,128)} copy(f32[16,256,1408]{2,1,0:T(8,128)} %param.5) | data formatting | bytes 46137344 | tf_op args[0]
  54.7 32.5 %all-reduce.3.cloned.1.call-done = (f32[16,1408]{1,0:T(8,128)}, f32[16,1408]{1,0:T(8,128)}, f32[16,1408]{1,0:T(8,128)}) async-done(((f32[16,1408]{1,0:T(8,128)}, f32[16,1408]{1,0:T(8,128)}, f32[16,1408]{1,0:T(8,128)}), (f32[16,1408]{1,0:T(8,128)}, f32[16,1408]{1,0:T(8,128)}, f32[16,1408]{1,0:T(8,128)})) %all-reduce.3.cloned.1.call-update) | async-done | bytes 270352 | tf_op jit(solution)/shard_map/pmax | solution.py:8
  87.2 1.1 copy.26
  88.4 14.2 %divide_convert_fusion.1 = bf16[16,256,1408]{1,0,2:T(8,128)(2,1)} fusion(f32[16,256,1408]{1,0,2:T(8,128)} %copy.27, f32[16,1408]{0,1:T(8,128)S(1)} %copy.26), kind=kLoop, calls=%fused_computation.5 | loop fusion | flops 11534336 | bytes 34693120 | tf_op jit(solution)/shard_map/convert_element_type | solution.py:17
  102.6 5.4 all-to-all-start
  108.0 0.0 copy-start
  108.0 23.7 %copy.31 = f32[16,256,1408]{1,0,2:T(8,128)} copy(f32[16,256,1408]{2,1,0:T(8,128)} %param.6) | data formatting | bytes 46137344 | tf_op args[1]
  131.7 0.0 copy-done
  131.7 0.3 copy.30
  132.0 0.0 copy-start.1
  132.0 14.2 %divide_convert_fusion = bf16[16,256,1408]{1,0,2:T(8,128)(2,1)} fusion(f32[16,256,1408]{1,0,2:T(8,128)} %copy.31, f32[16,1408]{0,1:T(8,128)S(1)} %copy.30), kind=kLoop, calls=%fused_computation.3 | loop fusion | flops 11534336 | bytes 34693120 | tf_op jit(solution)/shard_map/convert_element_type | solution.py:18
  146.2 213.1 %all-to-all-done = bf16[16,256,1408]{1,0,2:T(8,128)(2,1)} async-done(((bf16[16,256,1408]{1,0,2:T(8,128)(2,1)}), bf16[16,256,1408]{1,0,2:T(8,128)(2,1)}, u32[]{:S(2)}, u32[]{:S(2)}) %all-to-all-start) | async-done | bytes 11534368 | tf_op jit(solution)/shard_map/all_to_all | solution.py:22
  359.4 5.2 all-to-all-start.1
  364.6 0.0 copy-done.1
  364.6 0.3 copy.34
  364.9 0.0 copy-start.2
  364.9 0.0 copy-start.3
  364.9 32.6 %fusion = bf16[16,1408,256]{2,0,1:T(8,128)(2,1)} fusion(f32[16,1408,256]{2,1,0:T(8,128)} %param.7, f32[16,1408]{0,1:T(8,128)S(1)} %copy.34), kind=kLoop, calls=%fused_computation.1 | loop fusion | flops 11534336 | bytes 34693120 | tf_op jit(solution)/shard_map/convert_element_type | solution.py:19
  397.5 218.4 %all-to-all-done.1 = bf16[16,256,1408]{1,0,2:T(8,128)(2,1)} async-done(((bf16[16,256,1408]{1,0,2:T(8,128)(2,1)}), bf16[16,256,1408]{1,0,2:T(8,128)(2,1)}, u32[]{:S(2)}, u32[]{:S(2)}) %all-to-all-start.1) | async-done | bytes 11534368 | tf_op jit(solution)/shard_map/all_to_all | solution.py:23
  615.9 5.3 all-to-all-start.2
  621.2 0.0 copy-done.2
  621.2 0.0 copy-done.3
  621.3 257.3 %all_gather.9 = bf16[2048,16]{0,1:T(8,128)(2,1)S(1)} all-gather(bf16[256,16]{0,1:T(8,128)(2,1)S(1)} %multiply_convert_fusion), channel_id=1, replica_groups=mesh['ep'=4,'fsdp'=8] {'fsdp'}, dimensions={0}, use_global_device_ids=true | all-gather | bytes 73728 | tf_op jit(solution)/shard_map/all_gather | solution.py:36
  878.5 9.1 all-gather
  887.7 0.7 copy.45
  888.4 1.4 constant_dynamic-slice_fusion.2
  889.8 0.7 constant_dynamic-slice_fusion
  890.5 11.3 %copy.29 = bf16[16,8,256,176]{2,1,3,0:T(8,128)(2,1)} copy(bf16[16,8,256,176]{2,0,3,1:T(8,128)(2,1)} %bitcast.2) | data formatting | bytes 23068672 | tf_op jit(solution)/shard_map/all_to_all | solution.py:22
  901.8 18.0 %all_to_all.42 = bf16[16,2048,176]{1,2,0:T(8,128)(2,1)} reshape(bf16[16,8,256,176]{2,1,3,0:T(8,128)(2,1)} %copy.29) | data formatting | bytes 23068672 | tf_op jit(solution)/shard_map/all_to_all | solution.py:22
  919.8 11.3 %copy.33 = bf16[16,8,256,176]{2,1,3,0:T(8,128)(2,1)} copy(bf16[16,8,256,176]{2,0,3,1:T(8,128)(2,1)} %bitcast.5) | data formatting | bytes 23068672 | tf_op jit(solution)/shard_map/all_to_all | solution.py:23
  931.1 18.0 %all_to_all.46 = bf16[16,2048,176]{1,2,0:T(8,128)(2,1)} reshape(bf16[16,8,256,176]{2,1,3,0:T(8,128)(2,1)} %copy.33) | data formatting | bytes 23068672 | tf_op jit(solution)/shard_map/all_to_all | solution.py:23
  949.1 0.0 all-to-all-done.2
  949.1 11.4 %copy.36 = bf16[16,176,8,256]{3,2,1,0:T(8,128)(2,1)} copy(bf16[16,176,8,256]{3,0,1,2:T(8,128)(2,1)} %bitcast.7) | data formatting | bytes 23068672 | tf_op jit(solution)/shard_map/all_to_all | solution.py:25
  960.4 18.0 %all_to_all.50 = bf16[16,176,2048]{2,1,0:T(8,128)(2,1)} reshape(bf16[16,176,8,256]{3,2,1,0:T(8,128)(2,1)} %copy.36) | data formatting | bytes 23068672 | tf_op jit(solution)/shard_map/all_to_all | solution.py:25
  (2 shorter events, 0.0 us)
Async XLA Ops:
  7.2 80.1 %all-reduce.3.cloned.1.call-start = ((), (), s32[]{:S(2)}) async-start(), calls=%async_computation.3 | async-start | bytes 540672 | tf_op jit(solution)/shard_map/pmax | solution.py:8
  7.2 21.3 %slice-start = ((s8[23068672]{0:T(1024)(128)(4,1)}), s8[4194304]{0:T(1024)(128)(4,1)S(1)}, s32[]{:S(2)}) async-start(s8[23068672]{0:T(1024)(128)(4,1)} %bitcast.26), calls=%async_computation.4 | async-start | bytes 8388608
  7.2 21.3 %slice-start.1 = ((s8[23068672]{0:T(1024)(128)(4,1)}), s8[4194304]{0:T(1024)(128)(4,1)S(1)}, s32[]{:S(2)}) async-start(s8[23068672]{0:T(1024)(128)(4,1)} %bitcast.26), calls=%async_computation.5 | async-start | bytes 8388608
  7.2 21.3 %slice-start.2 = ((s8[23068672]{0:T(1024)(128)(4,1)}), s8[4194304]{0:T(1024)(128)(4,1)S(1)}, s32[]{:S(2)}) async-start(s8[23068672]{0:T(1024)(128)(4,1)} %bitcast.26), calls=%async_computation.6 | async-start | bytes 8388608
  17.7 10.8 %slice-start.3 = ((s8[23068672]{0:T(1024)(128)(4,1)}), s8[4194304]{0:T(1024)(128)(4,1)S(1)}, s32[]{:S(2)}) async-start(s8[23068672]{0:T(1024)(128)(4,1)} %bitcast.26), calls=%async_computation.7 | async-start | bytes 8388608
  17.7 10.8 %slice-start.4 = ((s8[23068672]{0:T(1024)(128)(4,1)}), s8[4194304]{0:T(1024)(128)(4,1)S(1)}, s32[]{:S(2)}) async-start(s8[23068672]{0:T(1024)(128)(4,1)} %bitcast.26), calls=%async_computation.8 | async-start | bytes 8388608
  17.7 10.9 %slice-start.5 = ((s8[23068672]{0:T(1024)(128)(4,1)}), s8[2097152]{0:T(1024)(128)(4,1)S(1)}, s32[]{:S(2)}) async-start(s8[23068672]{0:T(1024)(128)(4,1)} %bitcast.26), calls=%async_computation.9 | async-start | bytes 4194304
  102.6 256.8 %all-to-all-start = ((bf16[16,256,1408]{1,0,2:T(8,128)(2,1)}), bf16[16,256,1408]{1,0,2:T(8,128)(2,1)}, u32[]{:S(2)}, u32[]{:S(2)}) async-start(bf16[16,256,1408]{1,0,2:T(8,128)(2,1)} %divide_convert_fusion.1), calls=%async_computation | async-start | bytes 23068672 | tf_op jit(solution)/shard_map/all_to_all | solution.py:22
  108.0 23.7 %copy-start = (f32[16,1408]{1,0:T(8,128)S(1)}, f32[16,1408]{1,0:T(8,128)}, u32[]{:S(2)}) copy-start(f32[16,1408]{1,0:T(8,128)} %get-tuple-element.8) | copy-start | bytes 270340
  132.0 232.6 %copy-start.1 = (f32[16,1408]{1,0:T(8,128)S(1)}, f32[16,1408]{1,0:T(8,128)}, u32[]{:S(2)}) copy-start(f32[16,1408]{1,0:T(8,128)} %get-tuple-element.9) | copy-start | bytes 270340
  359.4 256.5 %all-to-all-start.1 = ((bf16[16,256,1408]{1,0,2:T(8,128)(2,1)}), bf16[16,256,1408]{1,0,2:T(8,128)(2,1)}, u32[]{:S(2)}, u32[]{:S(2)}) async-start(bf16[16,256,1408]{1,0,2:T(8,128)(2,1)} %divide_convert_fusion), calls=%async_computation.1 | async-start | bytes 23068672 | tf_op jit(solution)/shard_map/all_to_all | solution.py:23
  364.9 256.3 %copy-start.2 = (f32[256,16]{0,1:T(8,128)S(1)}, f32[256,16]{0,1:T(8,128)}, u32[]{:S(2)}) copy-start(f32[256,16]{0,1:T(8,128)} %param.8) | copy-start | bytes 49156
  364.9 256.3 %copy-start.3 = (f32[256]{0:T(256)S(1)}, f32[256]{0:T(256)}, u32[]{:S(2)}) copy-start(f32[256]{0:T(256)} %param.9) | copy-start | bytes 3076
  615.9 333.2 %all-to-all-start.2 = ((bf16[16,1408,256]{2,0,1:T(8,128)(2,1)}), bf16[16,1408,256]{2,0,1:T(8,128)(2,1)}, u32[]{:S(2)}, u32[]{:S(2)}) async-start(bf16[16,1408,256]{2,0,1:T(8,128)(2,1)} %fusion), calls=%async_computation.2 | async-start | bytes 23068672 | tf_op jit(solution)/shard_map/all_to_all | solution.py:25
Sparse Core Ops, SparseCore 0:
  31.1 56.0 all-reduce.2
